TPU v7x, 32 devices: a whole 2x2x4 slice. The times are simulated.
32 devices in a mesh: gy: 4 (over x, core), gx: 8 (over z, y).
Axes of the slice: x: 2, y: 2, z: 4, core: 2. Of those that a mesh axis runs over, the one named last changes fastest.
Arguments:
- first_factor: bfloat16 [4096, 2048], P('gy', 'gx'), may hold values from -6 to 6
- second_factor: bfloat16 [2048, 8192], P('gy', 'gx'), may hold values from -0.125 to 0.125
- result_in: float32 [4096, 8192], P('gy', 'gx'), may hold values from -6 to 6
- pivot_scale: float32 [2048], replicated, may hold values from 0.25 to 1.75
Outputs:
- corrected: float32 [4096, 8192], P('gy', 'gx')
All inputs are finite; a program needn't handle non-finite values.
Results may differ from a plain program's by a relative error of at most 0.002.
Values may be sent and summed in bfloat16 or wider, within the bound.
A program may use at most 128 MiB of HBM per device.

v0:
```python
import jax
import jax.numpy as jnp
from jax import lax
from jax.sharding import PartitionSpec as P


def join_panel(left_panel, right_panel):
    return jnp.dot(left_panel, right_panel, preferred_element_type=jnp.float32)


def shards(first_factor, second_factor, result_in, pivot_scale):
    share = first_factor.shape[1]
    part_scale = lax.dynamic_slice_in_dim(pivot_scale, lax.axis_index("gx") * share, share)
    scaled_left = (first_factor.astype(jnp.float32) * part_scale).astype(jnp.bfloat16)
    left_line = lax.all_gather(scaled_left, "gx", axis=1, tiled=True)
    total = join_panel(left_line, lax.all_gather(second_factor, "gy", axis=0, tiled=True))
    corrected = result_in - total
    row_power = lax.psum(jnp.sum(corrected * corrected, axis=1), "gx")
    corrected = (
        corrected
        * lax.rsqrt(row_power / (corrected.shape[1] * lax.axis_size("gx")) + 1e-06)[:, None]
    )
    return corrected


def solution(mesh):
    return jax.shard_map(
        shards,
        mesh=mesh,
        in_specs=(P("gy", "gx"), P("gy", "gx"), P("gy", "gx"), P()),
        out_specs=P("gy", "gx"),
        check_vma=False,
    )
```

profile of v0, /device:TPU:0, one launch (start us, length us, event | category | flops | bytes accessed | tf_op | source)
XLA Modules:
  0.0 169.9 jit_solution(15891152812098854044)
XLA Ops:
  6.5 0.0 all-gather.5.cloned.1.call-start
  6.5 0.7 all-gather.5.cloned.1.call-update
  7.3 0.0 all-gather.3.cloned.1.call-start
  7.3 0.8 dynamic_slice.3
  8.1 2.0 %multiply_convert_fusion = bf16[1024,256]{1,0:T(8,128)(2,1)} fusion(bf16[1024,256]{1,0:T(8,128)(2,1)} %param.4, f32[256]{0:T(256)S(1)} %dynamic_slice.3), kind=kLoop, calls=%fused_computation.3 | loop fusion | flops 786432 | bytes 1049600 | tf_op jit(solution)/shard_map/convert_element_type | solution.py:14
  10.1 0.0 all-gather.3.cloned.1.call-update
  10.1 5.3 %copy.5 = f32[1024,1024]{0,1:T(8,128)} copy(f32[1024,1024]{1,0:T(8,128)} %param.6) | data formatting | bytes 8388608 | tf_op args[2]
  15.4 30.7 %all-gather.5.cloned.1.call-done = bf16[2048,1024]{1,0:T(8,128)(2,1)} async-done(((bf16[512,1024]{1,0:T(8,128)(2,1)}), bf16[2048,1024]{1,0:T(8,128)(2,1)}) %all-gather.5.cloned.1.call-update) | async-done | bytes 4194320 | tf_op jit(solution)/shard_map/all_gather | solution.py:16
  46.1 76.7 %all-gather.3.cloned.1.call-done = bf16[1024,2048]{1,0:T(8,128)(2,1)} async-done(((bf16[1024,256]{1,0:T(8,128)(2,1)}), bf16[1024,2048]{1,0:T(8,128)(2,1)}) %all-gather.3.cloned.1.call-update) | async-done | bytes 4194320 | tf_op jit(solution)/shard_map/all_gather | solution.py:15
  122.8 11.3 %multiply_reduce_fusion = (f32[1024]{0:T(1024)S(1)}, f32[1024,1024]{0,1:T(8,128)}) fusion(f32[1024,1024]{0,1:T(8,128)} %copy.5, bf16[1024,2048]{1,0:T(8,128)(2,1)} %all-gather.3.cloned.1.call-done, bf16[2048,1024]{1,0:T(8,128)(2,1)} %all-gather.5.cloned.1.call-done), kind=kOutput, calls=%fused_computation | convolution fusion | flops 4298112000 | bytes 16781312 | tf_op jit(solution)/shard_map/dot_general | solution.py:8
  134.1 18.6 %psum.7 = f32[1024]{0:T(1024)S(1)} all-reduce(f32[1024]{0:T(1024)S(1)} %get-tuple-element.5), channel_id=1, replica_groups=mesh['gy'=4,'gx'=8] {'gx'}, use_global_device_ids=true, to_apply=%region_1.0 | all-reduce | flops 1024 | bytes 8192 | tf_op jit(solution)/shard_map/psum | solution.py:18
  152.7 5.0 %broadcast_multiply_fusion = f32[1024,1024]{0,1:T(8,128)} fusion(f32[1024,1024]{0,1:T(8,128)} %get-tuple-element.6, f32[1024]{0:T(1024)S(1)} %add_rsqrt_fusion), kind=kLoop, calls=%fused_computation.1 | loop fusion | flops 1048576 | bytes 8392704 | tf_op jit(solution)/shard_map/mul | solution.py:20
  157.7 5.3 %copy.6 = f32[1024,1024]{1,0:T(8,128)} copy(f32[1024,1024]{0,1:T(8,128)} %broadcast_multiply_fusion) | data formatting | bytes 8388608 | tf_op jit(solution)/shard_map/mul | solution.py:20
  (1 shorter events, 0.0 us)
Async XLA Ops:
  6.5 39.6 %all-gather.5.cloned.1.call-start = ((), (), s32[]{:S(2)}) async-start(), calls=%async_computation.1 | async-start | bytes 5242880 | tf_op jit(solution)/shard_map/all_gather | solution.py:16
  7.3 115.6 %all-gather.3.cloned.1.call-start = ((), (), s32[]{:S(2)}) async-start(), calls=%async_computation | async-start | bytes 4718592 | tf_op jit(solution)/shard_map/all_gather | solution.py:15
Sparse Core Ops, SparseCore 0:
  8.9 37.1 all-gather.4
  48.1 74.6 all-gather.2
where the time goes:
time: 170 us
  waiting for transfers between devices  108 us (64%)
  blocking collectives  18.6 us (11%)
  between operations  13.4 us (8%)
  local copies, waits for them, and re-layouts  11.4 us (7%)
  matrix products  11.3 us (7%)
  other arithmetic  6.98 us (4%)
    all_gather x1, waiting for transfers between devices, shards(): left_line = lax.all_gather(scaled_left, 'gx', axis=1, tiled=True)  76.7 us
    all_gather x1, waiting for transfers between devices, shards(): lax.all_gather(second_factor, 'gy', axis=0, tiled=True)  30.7 us
    psum x1, blocking collectives, shards(): row_power = lax.psum(jnp.sum(corrected * corrected, axis=1), 'gx')  18.6 us
    dot_general x1, matrix products, join_panel(): return jnp.dot(left_panel, right_panel, preferred_element_type=jnp.float32)  11.3 us
    unnamed x1, local copies, waits for them, and re-layouts  5.35 us
    mul x1, local copies, waits for them, and re-layouts, shards(): corrected * lax.rsqrt(row_power / (corrected.shape[1] * lax.axis_size('gx...  5.34 us
    mul x1, other arithmetic, shards(): corrected * lax.rsqrt(row_power / (corrected.shape[1] * lax.axis_size('gx...  4.98 us
  transfers between devices with their start and end apart: 2, of which 2 were waited for; matrix products, arithmetic and copies ran while one was open for 5% of the time, Pallas kernels for 0%

commit v1 on v0

v1 whole, which is shorter than its diff:
```python
import functools

import jax
import jax.numpy as jnp
from jax import lax
from jax.experimental import pallas as pl
from jax.experimental.pallas import tpu as pltpu
from jax.sharding import PartitionSpec as P

MESH = pl.DeviceIdType.MESH
LANES = 128


def kernel(n_gx, n_gy, a_ref, b_ref, r_ref, p_ref, o_ref, abuf, bbuf, pbuf, pv,
           a_loc, b_loc, r_loc, p_loc, arecv, brecv, zs, zd, ys, xs, bcs, bxs, psend, precv):
    half, ka = abuf.shape[2], abuf.shape[3]
    nc = b_ref.shape[0] // ka
    line, xn = n_gx // 2, n_gy // 2
    gx, gy = lax.axis_index("gx"), lax.axis_index("gy")
    z, y = gx // 2, gx % 2
    x, core = gy // 2, gy % 2
    pair = z + 1 - 2 * (z % 2)
    total_cols = o_ref.shape[1] * n_gx

    def blk(zz, yy):
        return zz * 2 + yy

    up = {"gx": blk(jnp.minimum(z + 1, line - 1), y), "gy": gy}
    down = {"gx": blk(jnp.maximum(z - 1, 0), y), "gy": gy}
    side = {"gx": blk(z, 1 - y), "gy": gy}
    across = {"gx": blk(pair, y), "gy": gy}
    mate = {"gx": gx, "gy": x * 2 + 1 - core}

    def x_peer(dx):
        return ((x + dx) % xn) * 2 + core

    a_in = [pltpu.make_async_copy(a_ref.at[pl.ds(h * half, half)], abuf.at[gx, h], a_loc.at[h]) for h in range(2)]
    b_in = [pltpu.make_async_copy(b_ref.at[pl.ds(c * ka, ka)], bbuf.at[gy * nc + c], b_loc.at[c]) for c in range(nc)]
    p_in = pltpu.make_async_copy(p_ref, pv, p_loc)
    r_in = pltpu.make_async_copy(r_ref, o_ref, r_loc)
    for cp in a_in + b_in + [p_in, r_in]:
        cp.start()

    barrier = pltpu.get_barrier_semaphore()
    for d in range(1, n_gx):
        pl.semaphore_signal(barrier, inc=1, device_id={"gx": (gx + d) % n_gx, "gy": gy}, device_id_type=MESH)
    pl.semaphore_signal(barrier, inc=1, device_id=mate, device_id_type=MESH)
    for dx in range(1, xn):
        pl.semaphore_signal(barrier, inc=1, device_id={"gx": gx, "gy": x_peer(dx)}, device_id_type=MESH)
    pl.semaphore_wait(barrier, n_gx - 1 + 1 + xn - 1)

    def acopy(j, h, sem, dev):
        return pltpu.make_async_remote_copy(
            src_ref=abuf.at[j, h], dst_ref=abuf.at[j, h], send_sem=sem,
            recv_sem=arecv.at[j, h], device_id=dev, device_id_type=MESH)

    def bcopy(j, sem, dev):
        return pltpu.make_async_remote_copy(
            src_ref=bbuf.at[j], dst_ref=bbuf.at[j], send_sem=sem,
            recv_sem=brecv.at[j], device_id=dev, device_id_type=MESH)

    def a_arrived(j, h):
        acopy(j, h, xs, side).wait_recv()

    def b_arrived(j):
        bcopy(j, xs, mate).wait_recv()

    def to_side(zz, h):
        return acopy(blk(zz, y), h, ys.at[zz, h], side)

    def to_up(zz, h):
        return acopy(blk(zz, y), h, zs.at[zz, h], up)

    def to_down(zz, h):
        return acopy(blk(zz, y), h, zs.at[zz, h], down)

    def own_down(h):
        return acopy(gx, h, zd.at[h], down)

    def to_across():
        return acopy(blk(z, 1 - y), 1, xs, across)

    def to_mate(j):
        return bcopy(j, bcs.at[j], mate)

    def to_x(dx, c):
        return bcopy(gy * nc + c, bxs.at[(dx - 1) * nc + c], {"gx": gx, "gy": x_peer(dx)})

    has_up, has_down = z + 1 < line, z > 0

    for h in range(2):
        a_in[h].wait()
        to_side(z, h).start()
        pl.when(has_up)(lambda h=h: to_up(z, h).start())
        pl.when(has_down)(lambda h=h: own_down(h).start())
    for c in range(nc):
        b_in[c].wait()
        for dx in range(1, xn):
            to_x(dx, c).start()
        to_mate(gy * nc + c).start()

    def z_round(s, h):
        @pl.when(z - s >= 0)
        def _():
            zz = z - s
            a_arrived(blk(zz, y), h)
            pl.when(has_up)(lambda: to_up(zz, h).start())
            if h == 0 or s > 1:
                to_side(zz, h).start()
            else:
                pl.when(zz != pair)(lambda: to_side(zz, h).start())

        @pl.when(z + s < line)
        def _():
            zz = z + s
            a_arrived(blk(zz, y), h)
            pl.when(has_down)(lambda: to_down(zz, h).start())
            if h == 0 or s > 1:
                to_side(zz, h).start()
            else:
                pl.when(zz != pair)(lambda: to_side(zz, h).start())

    def side_wait(zz, h, s):
        if h == 0 or s != 1:
            a_arrived(blk(zz, 1 - y), h)
        else:
            pl.when(zz != pair)(lambda: a_arrived(blk(zz, 1 - y), h))

    def y_round(s):
        for h in range(2):
            if s == 0:
                side_wait(z, h, s)
            else:
                pl.when(z - s >= 0)(lambda h=h: side_wait(z - s, h, s))
                pl.when(z + s < line)(lambda h=h: side_wait(z + s, h, s))

    def b_round(c):
        for dx in range(1, xn):
            j = x_peer(dx) * nc + c
            b_arrived(j)
            to_mate(j).start()

    def unit(j, h):
        rows = pl.ds(pl.multiple_of(h * half, half), half)
        scale = pv[:, pl.ds(pl.multiple_of(j * ka, ka), ka)]
        left = (abuf[j, h].astype(jnp.float32) * scale).astype(jnp.bfloat16)
        o_ref[rows, :] = o_ref[rows, :] - jnp.dot(left, bbuf[j], preferred_element_type=jnp.float32)

    def compute(yy, pred):
        def body(t, carry):
            zz, h = t // 2, t % 2
            pl.when(pred(zz, h))(lambda: unit(blk(zz, yy), h))
            return carry
        lax.fori_loop(0, 2 * line, body, 0)

    def near(zz, s):
        return jnp.logical_and(zz - z <= s, z - zz <= s)

    for s in range(1, line - 1):
        if s >= 2:
            y_round(s - 2)
        for h in range(2):
            z_round(s, h)
        if s - 1 < nc:
            b_round(s - 1)
    for c in range(line - 2, nc):
        b_round(c)
    to_across().start()
    for c in range(nc):
        b_arrived(mate["gy"] * nc + c)
        for dx in range(1, xn):
            b_arrived((((x + dx) % xn) * 2 + 1 - core) * nc + c)
    p_in.wait()
    r_in.wait()

    compute(y, lambda zz, h: near(zz, line - 2))
    z_round(line - 1, 0)
    y_round(line - 3)
    compute(1 - y, lambda zz, h: jnp.logical_and(near(zz, line - 3), jnp.logical_or(zz != pair, h == 0)))
    z_round(line - 1, 1)
    compute(y, lambda zz, h: jnp.logical_not(near(zz, line - 2)))

    def late(s, h, when=None):
        exists = jnp.logical_or(z >= s, z + s < line)
        zz = jnp.where(z >= s, z - s, z + s)

        @pl.when(exists if when is None else jnp.logical_and(exists, when))
        def _():
            a_arrived(blk(zz, 1 - y), h)
            unit(blk(zz, 1 - y), h)

    tiles = half // LANES
    lane_tiles = o_ref.shape[1] // LANES

    def pcopy(h, peer):
        return pltpu.make_async_remote_copy(
            src_ref=pbuf.at[h, gx], dst_ref=pbuf.at[h, gx], send_sem=psend.at[h],
            recv_sem=precv.at[h], device_id={"gx": peer, "gy": gy}, device_id_type=MESH)

    def power(h):
        found = []
        for r in range(tiles):
            block = o_ref[pl.ds(h * half + r * LANES, LANES), :]
            part = jnp.zeros((LANES, LANES), jnp.float32)
            for t in range(lane_tiles):
                piece = block[:, t * LANES:(t + 1) * LANES]
                part = part + piece * piece
            found.append(jnp.sum(part.T, axis=0, keepdims=True))
        spare = pbuf.shape[2] - tiles
        if spare:
            found.append(jnp.zeros((spare, LANES), jnp.float32))
        pbuf[h, gx] = jnp.concatenate(found, axis=0)
        for d in range(1, n_gx):
            pcopy(h, (gx + d) % n_gx).start()

    def settle(h):
        whole = pbuf.at[h, pl.ds(0, n_gx - 1)]
        pltpu.make_async_copy(whole, whole, precv.at[h]).wait()
        inv = lax.rsqrt(jnp.sum(pbuf[h], axis=0) / total_cols + 1e-06)
        for r in range(tiles):
            rows = pl.ds(h * half + r * LANES, LANES)
            col = jnp.broadcast_to(inv[r:r + 1, :], (LANES, LANES)).T
            for t in range(lane_tiles):
                cols = pl.ds(t * LANES, LANES)
                o_ref[rows, cols] = o_ref[rows, cols] * col

    is_end = jnp.logical_or(z == 0, z == line - 1)
    late(line - 2, 0)
    late(line - 2, 1, is_end)
    late(line - 1, 0)
    power(0)
    late(line - 2, 1, jnp.logical_not(is_end))
    late(line - 1, 1)
    a_arrived(blk(pair, 1 - y), 1)
    unit(blk(pair, 1 - y), 1)
    power(1)

    for h in range(2):
        to_side(z, h).wait_send()
        pl.when(has_up)(lambda h=h: to_up(z, h).wait_send())
        pl.when(has_down)(lambda h=h: own_down(h).wait_send())
    for s in range(1, line):
        for h in range(2):
            @pl.when(z - s >= 0)
            def _():
                pl.when(has_up)(lambda: to_up(z - s, h).wait_send())
                if h == 0 or s > 1:
                    to_side(z - s, h).wait_send()
                else:
                    pl.when(z - s != pair)(lambda: to_side(z - s, h).wait_send())

            @pl.when(z + s < line)
            def _():
                pl.when(has_down)(lambda: to_down(z + s, h).wait_send())
                if h == 0 or s > 1:
                    to_side(z + s, h).wait_send()
                else:
                    pl.when(z + s != pair)(lambda: to_side(z + s, h).wait_send())
    to_across().wait_send()
    for c in range(nc):
        to_mate(gy * nc + c).wait_send()
        for dx in range(1, xn):
            to_x(dx, c).wait_send()
            to_mate(x_peer(dx) * nc + c).wait_send()

    for h in range(2):
        settle(h)
    for h in range(2):
        whole = pbuf.at[h, pl.ds(0, n_gx - 1)]
        pltpu.make_async_copy(whole, whole, psend.at[h]).wait()


def solution(mesh):
    n_gx, n_gy = mesh.shape["gx"], mesh.shape["gy"]

    def shards(first_factor, second_factor, result_in, pivot_scale):
        rows, ka = first_factor.shape
        kb, cols = second_factor.shape
        inner = ka * n_gx
        half, nc, line, xn = rows // 2, kb // ka, n_gx // 2, n_gy // 2
        slot = -(-(half // LANES) // 8) * 8
        held = 2 * (rows * inner + inner * cols) + 4 * rows * cols
        dma = pltpu.SemaphoreType.DMA
        hbm = pl.BlockSpec(memory_space=pltpu.HBM)
        return pl.pallas_call(
            functools.partial(kernel, n_gx, n_gy),
            out_shape=jax.ShapeDtypeStruct((rows, cols), jnp.float32),
            in_specs=[hbm] * 4,
            out_specs=pl.BlockSpec(memory_space=pltpu.VMEM),
            scratch_shapes=[
                pltpu.VMEM((n_gx, 2, half, ka), jnp.bfloat16),
                pltpu.VMEM((n_gx, ka, cols), jnp.bfloat16),
                pltpu.VMEM((2, n_gx, slot, LANES), jnp.float32),
                pltpu.VMEM((1, inner), jnp.float32),
                dma((2,)), dma((nc,)), dma, dma,
                dma((n_gx, 2)), dma((n_gx,)),
                dma((line, 2)), dma((2,)), dma((line, 2)), dma,
                dma((n_gx,)), dma((max(xn - 1, 1) * nc,)),
                dma((2,)), dma((2,)),
            ],
            compiler_params=pltpu.CompilerParams(
                collective_id=0, has_side_effects=True, vmem_limit_bytes=held + 8 * 2**20),
        )(first_factor, second_factor, result_in, pivot_scale.reshape(1, inner))

    return jax.shard_map(
        shards,
        mesh=mesh,
        in_specs=(P("gy", "gx"), P("gy", "gx"), P("gy", "gx"), P()),
        out_specs=P("gy", "gx"),
        check_vma=False,
    )
```

time: 170 us -> 61.8 us (0.36)
  waiting for transfers between devices: 108 us -> 0 us
  Pallas kernels: 0 us -> 54.4 us
  blocking collectives: 18.6 us -> 0 us
  between operations: 13.4 us -> 0.01 us
  matrix products: 11.3 us -> 0 us
  other arithmetic: 6.98 us -> 0 us
  local copies, waits for them, and re-layouts: 11.4 us -> 7.16 us
    all_gather x2 -> x0, waiting for transfers between devices: 107 us -> none  [the longest x1 76.7 us: shards(): left_line = lax.all_gather(scaled_left, 'gx', axis=1, tiled=True)]
    pallas_call x0 -> x1, Pallas kernels: none -> 54.4 us  [shards(): pl.pallas_call(functools.partial(kernel, n_gx, n_gy), out_shape=jax.Shape...]
    psum x1 -> x0, blocking collectives: 18.6 us -> none  [shards(): row_power = lax.psum(jnp.sum(corrected * corrected, axis=1), 'gx')]
    dot_general x1 -> x0, matrix products: 11.3 us -> none  [join_panel(): return jnp.dot(left_panel, right_panel, preferred_element_type=jnp.float32)]
    mul x1 -> x0, local copies, waits for them, and re-layouts: 5.34 us -> none  [shards(): corrected * lax.rsqrt(row_power / (corrected.shape[1] * lax.axis_size('gx...]
    mul x1 -> x0, other arithmetic: 4.98 us -> none  [shards(): corrected * lax.rsqrt(row_power / (corrected.shape[1] * lax.axis_size('gx...]
    convert_element_type x1 -> x0, other arithmetic: 1.99 us -> none  [shards(): (first_factor.astype(jnp.float32) * part_scale).astype(jnp.bfloat16)]
    unnamed x1 -> x9, local copies, waits for them, and re-layouts: 5.35 us -> 7.16 us
  transfers between devices with their start and end apart: 2 -> 0, of which waited for: 2 -> 0; matrix products, arithmetic and copies ran while one was open for 5% -> 0% of each run, Pallas kernels for 0% -> 0%
where the time goes in v1:
time: 61.8 us; the launch traced here: 61.5 us
  Pallas kernels  54.4 us (88%)
  local copies, waits for them, and re-layouts  7.16 us (12%)
    pallas_call x1, Pallas kernels, shards(): pl.pallas_call(functools.partial(kernel, n_gx, n_gy), out_shape=jax.Shape...  54.4 us
    unnamed x9, local copies, waits for them, and re-layouts  7.16 us

profile of v1, /device:TPU:0, one launch (start us, length us, event | category | flops | bytes accessed | tf_op | source)
XLA Modules:
  0.0 61.5 jit_solution(14663798000754841953)
XLA Ops:
  0.0 0.0 copy-start
  0.0 2.2 %copy-done = f32[1024,1024]{1,0:T(8,128)S(1)} copy-done((f32[1024,1024]{1,0:T(8,128)S(1)}, f32[1024,1024]{1,0:T(8,128)}, u32[]{:S(2)}) %copy-start) | copy-done | bytes 4194328
  2.2 0.0 copy-start.1
  2.2 1.2 %copy-done.1 = bf16[512,1024]{1,0:T(8,128)(2,1)S(1)} copy-done((bf16[512,1024]{1,0:T(8,128)(2,1)S(1)}, bf16[512,1024]{1,0:T(8,128)(2,1)}, u32[]{:S(2)}) %copy-start.1) | copy-done | bytes 1048600
  3.4 0.0 copy-start.2
  3.4 1.0 %copy-done.2 = bf16[1024,256]{1,0:T(8,128)(2,1)S(1)} copy-done((bf16[1024,256]{1,0:T(8,128)(2,1)S(1)}, bf16[1024,256]{1,0:T(8,128)(2,1)}, u32[]{:S(2)}) %copy-start.2) | copy-done | bytes 524312
  4.5 0.0 copy-start.3
  4.5 0.7 %copy-done.3 = f32[2048]{0:T(1024)S(1)} copy-done((f32[2048]{0:T(1024)S(1)}, f32[2048]{0:T(1024)}, u32[]{:S(2)}) %copy-start.3) | copy-done | bytes 8216
  5.2 54.4 %shard_map.46 = f32[1024,1024]{1,0:T(8,128)S(1)} custom-call(bf16[1024,256]{1,0:T(8,128)(2,1)S(1)} %copy-done.2, bf16[512,1024]{1,0:T(8,128)(2,1)S(1)} %copy-done.1, f32[1024,1024]{1,0:T(8,128)S(1)} %copy-done, f32[1,2048]{1,0:T(1,128)S(1)} %bitcast.1), custom_call_target="tpu_custom_call" | custom-call | tf_op jit(solution)/shard_map/pallas_call | solution.py:285
  59.5 2.0 %copy.6 = f32[1024,1024]{1,0:T(8,128)} copy(f32[1024,1024]{1,0:T(8,128)S(1)} %shard_map.46) | data formatting | bytes 8388608
Async XLA Ops:
  0.0 2.2 %copy-start = (f32[1024,1024]{1,0:T(8,128)S(1)}, f32[1024,1024]{1,0:T(8,128)}, u32[]{:S(2)}) copy-start(f32[1024,1024]{1,0:T(8,128)} %r_ref.1) | copy-start | bytes 12582916
  2.2 1.2 %copy-start.1 = (bf16[512,1024]{1,0:T(8,128)(2,1)S(1)}, bf16[512,1024]{1,0:T(8,128)(2,1)}, u32[]{:S(2)}) copy-start(bf16[512,1024]{1,0:T(8,128)(2,1)} %b_ref.1) | copy-start | bytes 3145732
  3.4 1.0 %copy-start.2 = (bf16[1024,256]{1,0:T(8,128)(2,1)S(1)}, bf16[1024,256]{1,0:T(8,128)(2,1)}, u32[]{:S(2)}) copy-start(bf16[1024,256]{1,0:T(8,128)(2,1)} %a_ref.1) | copy-start | bytes 1572868
  4.5 0.7 %copy-start.3 = (f32[2048]{0:T(1024)S(1)}, f32[2048]{0:T(1024)}, u32[]{:S(2)}) copy-start(f32[2048]{0:T(1024)} %param.7) | copy-start | bytes 24580

commit v2 on v1

--- a/solution.py
+++ b/solution.py
@@ -9,11 +9,12 @@
 
 MESH = pl.DeviceIdType.MESH
 LANES = 128
+PARTS = 4
 
 
 def kernel(n_gx, n_gy, a_ref, b_ref, r_ref, p_ref, o_ref, abuf, bbuf, pbuf, pv,
            a_loc, b_loc, r_loc, p_loc, arecv, brecv, zs, zd, ys, xs, bcs, bxs, psend, precv):
-    half, ka = abuf.shape[2], abuf.shape[3]
+    part, ka = abuf.shape[2], abuf.shape[3]
     nc = b_ref.shape[0] // ka
     line, xn = n_gx // 2, n_gy // 2
     gx, gy = lax.axis_index("gx"), lax.axis_index("gy")
@@ -34,7 +35,7 @@
     def x_peer(dx):
         return ((x + dx) % xn) * 2 + core
 
-    a_in = [pltpu.make_async_copy(a_ref.at[pl.ds(h * half, half)], abuf.at[gx, h], a_loc.at[h]) for h in range(2)]
+    a_in = [pltpu.make_async_copy(a_ref.at[pl.ds(h * part, part)], abuf.at[gx, h], a_loc.at[h]) for h in range(PARTS)]
     b_in = [pltpu.make_async_copy(b_ref.at[pl.ds(c * ka, ka)], bbuf.at[gy * nc + c], b_loc.at[c]) for c in range(nc)]
     p_in = pltpu.make_async_copy(p_ref, pv, p_loc)
     r_in = pltpu.make_async_copy(r_ref, o_ref, r_loc)
@@ -60,10 +61,10 @@
             recv_sem=brecv.at[j], device_id=dev, device_id_type=MESH)
 
     def a_arrived(j, h):
-        acopy(j, h, xs, side).wait_recv()
+        acopy(j, h, xs.at[0], side).wait_recv()
 
     def b_arrived(j):
-        bcopy(j, xs, mate).wait_recv()
+        bcopy(j, xs.at[0], mate).wait_recv()
 
     def to_side(zz, h):
         return acopy(blk(zz, y), h, ys.at[zz, h], side)
@@ -77,8 +78,8 @@
     def own_down(h):
         return acopy(gx, h, zd.at[h], down)
 
-    def to_across():
-        return acopy(blk(z, 1 - y), 1, xs, across)
+    def to_across(h):
+        return acopy(blk(z, 1 - y), h, xs.at[h], across)
 
     def to_mate(j):
         return bcopy(j, bcs.at[j], mate)
@@ -88,7 +89,7 @@
 
     has_up, has_down = z + 1 < line, z > 0
 
-    for h in range(2):
+    for h in range(PARTS):
         a_in[h].wait()
         to_side(z, h).start()
         pl.when(has_up)(lambda h=h: to_up(z, h).start())
@@ -105,7 +106,7 @@
             zz = z - s
             a_arrived(blk(zz, y), h)
             pl.when(has_up)(lambda: to_up(zz, h).start())
-            if h == 0 or s > 1:
+            if h < PARTS // 2 or s > 1:
                 to_side(zz, h).start()
             else:
                 pl.when(zz != pair)(lambda: to_side(zz, h).start())
@@ -115,19 +116,19 @@
             zz = z + s
             a_arrived(blk(zz, y), h)
             pl.when(has_down)(lambda: to_down(zz, h).start())
-            if h == 0 or s > 1:
+            if h < PARTS // 2 or s > 1:
                 to_side(zz, h).start()
             else:
                 pl.when(zz != pair)(lambda: to_side(zz, h).start())
 
     def side_wait(zz, h, s):
-        if h == 0 or s != 1:
+        if h < PARTS // 2 or s != 1:
             a_arrived(blk(zz, 1 - y), h)
         else:
             pl.when(zz != pair)(lambda: a_arrived(blk(zz, 1 - y), h))
 
     def y_round(s):
-        for h in range(2):
+        for h in range(PARTS):
             if s == 0:
                 side_wait(z, h, s)
             else:
@@ -140,18 +141,19 @@
             b_arrived(j)
             to_mate(j).start()
 
-    def unit(j, h):
-        rows = pl.ds(pl.multiple_of(h * half, half), half)
+    def unit(j, h, n):
+        rows = pl.ds(pl.multiple_of(h * part, part), n * part)
         scale = pv[:, pl.ds(pl.multiple_of(j * ka, ka), ka)]
-        left = (abuf[j, h].astype(jnp.float32) * scale).astype(jnp.bfloat16)
+        left = abuf[j, pl.ds(h, n)].reshape(n * part, ka).astype(jnp.float32)
+        left = (left * scale).astype(jnp.bfloat16)
         o_ref[rows, :] = o_ref[rows, :] - jnp.dot(left, bbuf[j], preferred_element_type=jnp.float32)
 
-    def compute(yy, pred):
+    def compute(yy, pred, first=0, steps=2):
         def body(t, carry):
-            zz, h = t // 2, t % 2
-            pl.when(pred(zz, h))(lambda: unit(blk(zz, yy), h))
+            zz, h = t // steps, first + t % steps
+            pl.when(pred(zz, h))(lambda: unit(blk(zz, yy), h * (PARTS // 2), PARTS // 2))
             return carry
-        lax.fori_loop(0, 2 * line, body, 0)
+        lax.fori_loop(0, steps * line, body, 0)
 
     def near(zz, s):
         return jnp.logical_and(zz - z <= s, z - zz <= s)
@@ -159,13 +161,14 @@
     for s in range(1, line - 1):
         if s >= 2:
             y_round(s - 2)
-        for h in range(2):
+        for h in range(PARTS):
             z_round(s, h)
         if s - 1 < nc:
             b_round(s - 1)
     for c in range(line - 2, nc):
         b_round(c)
-    to_across().start()
+    for h in range(PARTS // 2, PARTS):
+        to_across(h).start()
     for c in range(nc):
         b_arrived(mate["gy"] * nc + c)
         for dx in range(1, xn):
@@ -173,23 +176,28 @@
     p_in.wait()
     r_in.wait()
 
-    compute(y, lambda zz, h: near(zz, line - 2))
     z_round(line - 1, 0)
+    compute(y, lambda zz, h: near(zz, line - 2), 0, 1)
+    z_round(line - 1, 1)
+    compute(y, lambda zz, h: near(zz, line - 2), 1, 1)
+    z_round(line - 1, 2)
     y_round(line - 3)
     compute(1 - y, lambda zz, h: jnp.logical_and(near(zz, line - 3), jnp.logical_or(zz != pair, h == 0)))
-    z_round(line - 1, 1)
+    z_round(line - 1, 3)
     compute(y, lambda zz, h: jnp.logical_not(near(zz, line - 2)))
 
-    def late(s, h, when=None):
-        exists = jnp.logical_or(z >= s, z + s < line)
+    is_end = jnp.logical_or(z == 0, z == line - 1)
+
+    def late(s, h, n, when=True):
         zz = jnp.where(z >= s, z - s, z + s)
 
-        @pl.when(exists if when is None else jnp.logical_and(exists, when))
+        @pl.when(jnp.logical_and(jnp.logical_or(z >= s, z + s < line), when))
         def _():
-            a_arrived(blk(zz, 1 - y), h)
-            unit(blk(zz, 1 - y), h)
-
-    tiles = half // LANES
+            for i in range(n):
+                a_arrived(blk(zz, 1 - y), h + i)
+            unit(blk(zz, 1 - y), h, n)
+
+    tiles = part // LANES
     lane_tiles = o_ref.shape[1] // LANES
 
     def pcopy(h, peer):
@@ -200,12 +208,12 @@
     def power(h):
         found = []
         for r in range(tiles):
-            block = o_ref[pl.ds(h * half + r * LANES, LANES), :]
-            part = jnp.zeros((LANES, LANES), jnp.float32)
+            block = o_ref[pl.ds(h * part + r * LANES, LANES), :]
+            acc = jnp.zeros((LANES, LANES), jnp.float32)
             for t in range(lane_tiles):
                 piece = block[:, t * LANES:(t + 1) * LANES]
-                part = part + piece * piece
-            found.append(jnp.sum(part.T, axis=0, keepdims=True))
+                acc = acc + piece * piece
+            found.append(jnp.sum(acc.T, axis=0, keepdims=True))
         spare = pbuf.shape[2] - tiles
         if spare:
             found.append(jnp.zeros((spare, LANES), jnp.float32))
@@ -218,33 +226,34 @@
         pltpu.make_async_copy(whole, whole, precv.at[h]).wait()
         inv = lax.rsqrt(jnp.sum(pbuf[h], axis=0) / total_cols + 1e-06)
         for r in range(tiles):
-            rows = pl.ds(h * half + r * LANES, LANES)
+            rows = pl.ds(h * part + r * LANES, LANES)
             col = jnp.broadcast_to(inv[r:r + 1, :], (LANES, LANES)).T
             for t in range(lane_tiles):
                 cols = pl.ds(t * LANES, LANES)
                 o_ref[rows, cols] = o_ref[rows, cols] * col
 
-    is_end = jnp.logical_or(z == 0, z == line - 1)
-    late(line - 2, 0)
-    late(line - 2, 1, is_end)
-    late(line - 1, 0)
-    power(0)
-    late(line - 2, 1, jnp.logical_not(is_end))
-    late(line - 1, 1)
-    a_arrived(blk(pair, 1 - y), 1)
-    unit(blk(pair, 1 - y), 1)
-    power(1)
-
-    for h in range(2):
+    for h in range(0, PARTS, PARTS // 2):
+        late(line - 2, h, PARTS // 2, is_end)
+    for h in range(PARTS):
+        late(jnp.where(is_end, line - 1, line - 2), h, 1)
+        if h >= PARTS // 2:
+            a_arrived(blk(pair, 1 - y), h)
+            unit(blk(pair, 1 - y), h, 1)
+        power(h)
+
+    for h in range(PARTS):
+        settle(h)
+
+    for h in range(PARTS):
         to_side(z, h).wait_send()
         pl.when(has_up)(lambda h=h: to_up(z, h).wait_send())
         pl.when(has_down)(lambda h=h: own_down(h).wait_send())
     for s in range(1, line):
-        for h in range(2):
+        for h in range(PARTS):
             @pl.when(z - s >= 0)
             def _():
                 pl.when(has_up)(lambda: to_up(z - s, h).wait_send())
-                if h == 0 or s > 1:
+                if h < PARTS // 2 or s > 1:
                     to_side(z - s, h).wait_send()
                 else:
                     pl.when(z - s != pair)(lambda: to_side(z - s, h).wait_send())
@@ -252,20 +261,19 @@
             @pl.when(z + s < line)
             def _():
                 pl.when(has_down)(lambda: to_down(z + s, h).wait_send())
-                if h == 0 or s > 1:
+                if h < PARTS // 2 or s > 1:
                     to_side(z + s, h).wait_send()
                 else:
                     pl.when(z + s != pair)(lambda: to_side(z + s, h).wait_send())
-    to_across().wait_send()
+    for h in range(PARTS // 2, PARTS):
+        to_across(h).wait_send()
     for c in range(nc):
         to_mate(gy * nc + c).wait_send()
         for dx in range(1, xn):
             to_x(dx, c).wait_send()
             to_mate(x_peer(dx) * nc + c).wait_send()
 
-    for h in range(2):
-        settle(h)
-    for h in range(2):
+    for h in range(PARTS):
         whole = pbuf.at[h, pl.ds(0, n_gx - 1)]
         pltpu.make_async_copy(whole, whole, psend.at[h]).wait()
 
@@ -277,8 +285,8 @@
         rows, ka = first_factor.shape
         kb, cols = second_factor.shape
         inner = ka * n_gx
-        half, nc, line, xn = rows // 2, kb // ka, n_gx // 2, n_gy // 2
-        slot = -(-(half // LANES) // 8) * 8
+        part, nc, line, xn = rows // PARTS, kb // ka, n_gx // 2, n_gy // 2
+        slot = -(-(part // LANES) // 8) * 8
         held = 2 * (rows * inner + inner * cols) + 4 * rows * cols
         dma = pltpu.SemaphoreType.DMA
         hbm = pl.BlockSpec(memory_space=pltpu.HBM)
@@ -288,19 +296,19 @@
             in_specs=[hbm] * 4,
             out_specs=pl.BlockSpec(memory_space=pltpu.VMEM),
             scratch_shapes=[
-                pltpu.VMEM((n_gx, 2, half, ka), jnp.bfloat16),
+                pltpu.VMEM((n_gx, PARTS, part, ka), jnp.bfloat16),
                 pltpu.VMEM((n_gx, ka, cols), jnp.bfloat16),
-                pltpu.VMEM((2, n_gx, slot, LANES), jnp.float32),
+                pltpu.VMEM((PARTS, n_gx, slot, LANES), jnp.float32),
                 pltpu.VMEM((1, inner), jnp.float32),
-                dma((2,)), dma((nc,)), dma, dma,
-                dma((n_gx, 2)), dma((n_gx,)),
-                dma((line, 2)), dma((2,)), dma((line, 2)), dma,
+                dma((PARTS,)), dma((nc,)), dma, dma,
+                dma((n_gx, PARTS)), dma((n_gx,)),
+                dma((line, PARTS)), dma((PARTS,)), dma((line, PARTS)), dma((PARTS,)),
                 dma((n_gx,)), dma((max(xn - 1, 1) * nc,)),
-                dma((2,)), dma((2,)),
+                dma((PARTS,)), dma((PARTS,)),
             ],
             compiler_params=pltpu.CompilerParams(
                 collective_id=0, has_side_effects=True, vmem_limit_bytes=held + 8 * 2**20),
-        )(first_factor, second_factor, result_in, pivot_scale.reshape(1, inner))
+        )(*[pltpu.with_memory_space_constraint(v, pltpu.HBM) for v in (first_factor, second_factor, result_in, pivot_scale.reshape(1, inner))])
 
     return jax.shard_map(
         shards,

time: 61.8 us -> 54.3 us (0.88)
  local copies, waits for them, and re-layouts: 7.16 us -> 2.02 us
  Pallas kernels: 54.4 us -> 52.1 us
    unnamed x9 -> x1, local copies, waits for them, and re-layouts: 7.16 us -> 2.02 us
    pallas_call x1, Pallas kernels: 54.4 us -> 52.1 us  [shards(): pl.pallas_call(functools.partial(kernel, n_gx, n_gy), out_shape=jax.Shape...]
where the time goes in v2:
time: 54.3 us; the launch traced here: 54.1 us
  Pallas kernels  52.1 us (96%)
  local copies, waits for them, and re-layouts  2.02 us (4%)
    pallas_call x1, Pallas kernels, shards(): pl.pallas_call(functools.partial(kernel, n_gx, n_gy), out_shape=jax.Shape...  52.1 us
    unnamed x1, local copies, waits for them, and re-layouts  2.02 us

profile of v2, /device:TPU:0, one launch (start us, length us, event | category | flops | bytes accessed | tf_op | source)
XLA Modules:
  0.0 54.1 jit_solution(12893781132118832559)
XLA Ops:
  0.0 52.1 %shard_map.46 = f32[1024,1024]{1,0:T(8,128)S(1)} custom-call(bf16[1024,256]{1,0:T(8,128)(2,1)} %a_ref.1, bf16[512,1024]{1,0:T(8,128)(2,1)} %b_ref.1, f32[1024,1024]{1,0:T(8,128)} %r_ref.1, f32[1,2048]{1,0:T(1,128)} %bitcast.1), custom_call_target="tpu_custom_call" | custom-call | tf_op jit(solution)/shard_map/pallas_call | solution.py:293
  52.1 2.0 %copy.6 = f32[1024,1024]{1,0:T(8,128)} copy(f32[1024,1024]{1,0:T(8,128)S(1)} %shard_map.46) | data formatting | bytes 8388608

commit v3 on v2

--- a/solution.py
+++ b/solution.py
@@ -35,6 +35,19 @@
     def x_peer(dx):
         return ((x + dx) % xn) * 2 + core
 
+    has_up, has_down = z + 1 < line, z > 0
+    barrier = pltpu.get_barrier_semaphore()
+
+    def greet(dev):
+        pl.semaphore_signal(barrier, inc=1, device_id=dev, device_id_type=MESH)
+
+    pl.when(has_up)(lambda: greet(up))
+    pl.when(has_down)(lambda: greet(down))
+    greet(side)
+    for dx in range(1, xn):
+        greet({"gx": gx, "gy": x_peer(dx)})
+    greet(mate)
+
     a_in = [pltpu.make_async_copy(a_ref.at[pl.ds(h * part, part)], abuf.at[gx, h], a_loc.at[h]) for h in range(PARTS)]
     b_in = [pltpu.make_async_copy(b_ref.at[pl.ds(c * ka, ka)], bbuf.at[gy * nc + c], b_loc.at[c]) for c in range(nc)]
     p_in = pltpu.make_async_copy(p_ref, pv, p_loc)
@@ -42,13 +55,7 @@
     for cp in a_in + b_in + [p_in, r_in]:
         cp.start()
 
-    barrier = pltpu.get_barrier_semaphore()
-    for d in range(1, n_gx):
-        pl.semaphore_signal(barrier, inc=1, device_id={"gx": (gx + d) % n_gx, "gy": gy}, device_id_type=MESH)
-    pl.semaphore_signal(barrier, inc=1, device_id=mate, device_id_type=MESH)
-    for dx in range(1, xn):
-        pl.semaphore_signal(barrier, inc=1, device_id={"gx": gx, "gy": x_peer(dx)}, device_id_type=MESH)
-    pl.semaphore_wait(barrier, n_gx - 1 + 1 + xn - 1)
+    pl.semaphore_wait(barrier, 2 + xn - 1 + has_up.astype(jnp.int32) + has_down.astype(jnp.int32))
 
     def acopy(j, h, sem, dev):
         return pltpu.make_async_remote_copy(
@@ -86,8 +93,6 @@
 
     def to_x(dx, c):
         return bcopy(gy * nc + c, bxs.at[(dx - 1) * nc + c], {"gx": gx, "gy": x_peer(dx)})
-
-    has_up, has_down = z + 1 < line, z > 0
 
     for h in range(PARTS):
         a_in[h].wait()

time: 54.3 us -> 54.1 us (level)
  no operation moved by 1% of the time
where the time goes in v3:
time: 54.1 us; the launch traced here: 54 us
  Pallas kernels  52 us (96%)
  local copies, waits for them, and re-layouts  2.02 us (4%)
    pallas_call x1, Pallas kernels, shards(): pl.pallas_call(functools.partial(kernel, n_gx, n_gy), out_shape=jax.Shape...  52 us
    unnamed x1, local copies, waits for them, and re-layouts  2.02 us

profile of v3, /device:TPU:0, one launch (start us, length us, event | category | flops | bytes accessed | tf_op | source)
XLA Modules:
  0.0 54.0 jit_solution(14445706213109043555)
XLA Ops:
  0.0 52.0 %shard_map.46 = f32[1024,1024]{1,0:T(8,128)S(1)} custom-call(bf16[1024,256]{1,0:T(8,128)(2,1)} %a_ref.1, bf16[512,1024]{1,0:T(8,128)(2,1)} %b_ref.1, f32[1024,1024]{1,0:T(8,128)} %r_ref.1, f32[1,2048]{1,0:T(1,128)} %bitcast.1), custom_call_target="tpu_custom_call" | custom-call | tf_op jit(solution)/shard_map/pallas_call | solution.py:298
  52.0 2.0 %copy.6 = f32[1024,1024]{1,0:T(8,128)} copy(f32[1024,1024]{1,0:T(8,128)S(1)} %shard_map.46) | data formatting | bytes 8388608

commit v4 on v3

--- a/solution.py
+++ b/solution.py
@@ -101,6 +101,8 @@
         pl.when(has_down)(lambda h=h: own_down(h).start())
     for c in range(nc):
         b_in[c].wait()
+    for i in range(nc):
+        c = (i + y) % nc
         for dx in range(1, xn):
             to_x(dx, c).start()
         to_mate(gy * nc + c).start()
@@ -140,7 +142,8 @@
                 pl.when(z - s >= 0)(lambda h=h: side_wait(z - s, h, s))
                 pl.when(z + s < line)(lambda h=h: side_wait(z + s, h, s))
 
-    def b_round(c):
+    def b_round(i):
+        c = (i + y) % nc
         for dx in range(1, xn):
             j = x_peer(dx) * nc + c
             b_arrived(j)
@@ -162,6 +165,17 @@
 
     def near(zz, s):
         return jnp.logical_and(zz - z <= s, z - zz <= s)
+
+    def b_settled(i):
+        c = (i + y) % nc
+        b_arrived(mate["gy"] * nc + c)
+        for dx in range(1, xn):
+            b_arrived((((x + dx) % xn) * 2 + 1 - core) * nc + c)
+
+    early = nc == 2
+
+    def rest(zz):
+        return jnp.logical_and(near(zz, line - 2), jnp.logical_not(near(zz, 1))) if early else near(zz, line - 2)
 
     for s in range(1, line - 1):
         if s >= 2:
@@ -170,21 +184,25 @@
             z_round(s, h)
         if s - 1 < nc:
             b_round(s - 1)
+        if s == 1 and early:
+            b_settled(0)
+            p_in.wait()
+            r_in.wait()
+            compute(y, lambda zz, h: near(zz, 1))
     for c in range(line - 2, nc):
         b_round(c)
     for h in range(PARTS // 2, PARTS):
         to_across(h).start()
-    for c in range(nc):
-        b_arrived(mate["gy"] * nc + c)
-        for dx in range(1, xn):
-            b_arrived((((x + dx) % xn) * 2 + 1 - core) * nc + c)
-    p_in.wait()
-    r_in.wait()
+    for i in range(1 if early else 0, nc):
+        b_settled(i)
+    if not early:
+        p_in.wait()
+        r_in.wait()
 
     z_round(line - 1, 0)
-    compute(y, lambda zz, h: near(zz, line - 2), 0, 1)
+    compute(y, lambda zz, h: rest(zz), 0, 1)
     z_round(line - 1, 1)
-    compute(y, lambda zz, h: near(zz, line - 2), 1, 1)
+    compute(y, lambda zz, h: rest(zz), 1, 1)
     z_round(line - 1, 2)
     y_round(line - 3)
     compute(1 - y, lambda zz, h: jnp.logical_and(near(zz, line - 3), jnp.logical_or(zz != pair, h == 0)))

time: 54.1 us -> 54.6 us (level)
  no operation moved by 1% of the time
where the time goes in v4:
time: 54.6 us; the launch traced here: 54.5 us
  Pallas kernels  52.4 us (96%)
  local copies, waits for them, and re-layouts  2.02 us (4%)
    pallas_call x1, Pallas kernels, shards(): pl.pallas_call(functools.partial(kernel, n_gx, n_gy), out_shape=jax.Shape...  52.4 us
    unnamed x1, local copies, waits for them, and re-layouts  2.02 us

profile of v4, /device:TPU:0, one launch (start us, length us, event | category | flops | bytes accessed | tf_op | source)
XLA Modules:
  0.0 54.5 jit_solution(14375427286633962621)
XLA Ops:
  0.0 52.4 %shard_map.46 = f32[1024,1024]{1,0:T(8,128)S(1)} custom-call(bf16[1024,256]{1,0:T(8,128)(2,1)} %a_ref.1, bf16[512,1024]{1,0:T(8,128)(2,1)} %b_ref.1, f32[1024,1024]{1,0:T(8,128)} %r_ref.1, f32[1,2048]{1,0:T(1,128)} %bitcast.1), custom_call_target="tpu_custom_call" | custom-call | tf_op jit(solution)/shard_map/pallas_call | solution.py:316
  52.4 2.0 %copy.6 = f32[1024,1024]{1,0:T(8,128)} copy(f32[1024,1024]{1,0:T(8,128)S(1)} %shard_map.46) | data formatting | bytes 8388608
